TPU v7x, 256 devices: a whole 4x4x8 slice. The times are simulated.
256 devices in a mesh: layer: 8 (over y, z_lo), lat: 4 (over x), tok: 8 (over z_hi, core).
Axes of the slice: x: 4, y: 4, z: 8 (z_hi: 4, z_lo: 2; z = z_hi * 2 + z_lo), core: 2. Of those that a mesh axis runs over, the one named last changes fastest.
Arguments:
- mlp_inputs: bfloat16 [8, 768, 4096], P('layer', ('lat', 'tok')), may hold values from -6 to 6
- mlp_outputs: bfloat16 [8, 768, 4096], P('layer', ('lat', 'tok')), may hold values from -6 to 6
- encoder: bfloat16 [8, 4096, 16384], P('layer', None, ('lat', 'tok')), may hold values from -0.09375 to 0.09375
- encoder_bias: float32 [8, 16384], P('layer', ('lat', 'tok')), may hold values from -3 to 3
- active_words: int32 [8, 768, 1024], P('layer', None, ('lat', 'tok')), may hold values from 0 to 65535
- decoder: bfloat16 [8, 16384, 4096], P('layer', ('lat', 'tok')), may hold values from -0.0234375 to 0.0234375
Outputs:
- reconstruction_error: bfloat16 [8, 768, 4096], P('layer', ('lat', 'tok'))
- decoder_grad: bfloat16 [8, 16384, 4096], P('layer', ('lat', 'tok'))
Inputs may be any that keep to these rules, and one draw needn't show every extreme that they name: `active_words`: each word holds 16 independent gate decisions of one token in its low 16 bits.
All inputs are finite; a program needn't handle non-finite values.
Results may differ from a plain program's by a relative error of at most 0.0037.
Values may be sent and summed in bfloat16 or wider, within the bound.
No kernel may reach another device: no remote copies, remote signals or barrier semaphores. Data moves between devices by JAX's collectives and lax.ppermute only.
A program may use at most 128 MiB of HBM per device.

v0:
```python
import jax
import jax.numpy as jnp
from jax import lax
from jax.sharding import Mesh
from jax.sharding import PartitionSpec as P

LAYER = ("layer_0", "layer_1")


def whole_of(x, axes, dim):
    if not axes:
        return x
    nearer = lax.all_gather(x, axes[-1], axis=dim, tiled=True)
    return whole_of(nearer, axes[:-1], dim)


def unpack_words(words):
    shifts = jnp.arange(16, dtype=jnp.int32)
    bits = jnp.right_shift(words[..., None], shifts) & 1
    return bits.reshape(words.shape[:-1] + (words.shape[-1] * 16,)).astype(jnp.float32)


def local(mlp_inputs, mlp_outputs, encoder, encoder_bias, active_words, decoder):
    weights_in = encoder[0]
    bias_row = encoder_bias[0]
    words = active_words[0]
    weights_out = decoder[0]
    before_gate = (
        jnp.dot(
            lax.all_gather(mlp_inputs[0], ("lat", "tok"), axis=0, tiled=True),
            weights_in,
            preferred_element_type=jnp.float32,
        )
        + bias_row[None, :]
    )
    latent = (unpack_words(words) * before_gate).astype(jnp.bfloat16)
    write = lax.psum_scatter(
        jnp.dot(latent, weights_out, preferred_element_type=jnp.float32),
        ("lat", "tok"),
        scatter_dimension=0,
        tiled=True,
    )
    target = mlp_outputs[0].astype(jnp.float32)
    layer_index = lax.axis_index(LAYER)
    piece = whole_of(write[None], LAYER, 0)
    levels = jnp.arange(piece.shape[0], dtype=jnp.int32)
    keep = (levels <= layer_index).astype(jnp.float32)
    recon = jnp.sum(piece * keep[:, None, None], axis=0)
    difference = recon - target
    piece = lax.all_gather(difference[None], LAYER, axis=0, tiled=True)
    levels = jnp.arange(piece.shape[0], dtype=jnp.int32)
    keep = (levels >= layer_index).astype(jnp.float32)
    later = jnp.sum(piece * keep[:, None, None], axis=0)
    signal = later.astype(jnp.bfloat16)
    tokens_all = latent.shape[0]
    gathered = lax.all_gather(signal, ("lat", "tok"), axis=0, tiled=True)
    total = lax.dot_general(
        latent, gathered, (((0,), (0,)), ((), ())), preferred_element_type=jnp.float32
    )
    grad_block = (total / tokens_all).astype(jnp.bfloat16)
    return (difference.astype(jnp.bfloat16)[None], grad_block[None])


def solution(mesh):
    split = Mesh(
        mesh.devices.reshape(4, 2, mesh.shape["lat"], mesh.shape["tok"]),
        ("layer_0", "layer_1", "lat", "tok"),
    )
    placed = (
        P(LAYER, ("lat", "tok"), None),
        P(LAYER, ("lat", "tok"), None),
        P(LAYER, None, ("lat", "tok")),
        P(LAYER, ("lat", "tok")),
        P(LAYER, None, ("lat", "tok")),
        P(LAYER, ("lat", "tok"), None),
    )
    return jax.shard_map(
        local,
        mesh=split,
        in_specs=placed,
        out_specs=(P(LAYER, ("lat", "tok"), None), P(LAYER, ("lat", "tok"), None)),
        check_vma=False,
    )
```

profile of v0, /device:TPU:1, one launch (start us, length us, event | category | flops | bytes accessed | tf_op | source)
XLA Modules:
  0.0 454.7 jit_solution(15112110966650471053)
XLA Ops:
  7.2 0.0 copy-start.2
  7.2 0.0 all-gather.13.cloned.1.call-start
  7.2 0.7 all-gather.13.cloned.1.call-update
  7.9 0.0 reduce-scatter.2.cloned.1.call-start
  8.0 1.0 shift_right_arithmetic.23
  9.0 0.5 copy.10
  9.5 0.1 shift_right_arithmetic.26
  9.5 74.2 %all-gather.13.cloned.1.call-done = bf16[1,768,4096]{2,1,0:T(8,128)(2,1)} async-done(((bf16[1,24,4096]{2,1,0:T(8,128)(2,1)}), bf16[1,768,4096]{2,1,0:T(8,128)(2,1)}) %all-gather.13.cloned.1.call-update) | async-done | bytes 6291472 | tf_op jit(solution)/shard_map/all_gather | solution.py:30
  83.7 0.0 copy-done.2
  83.7 0.0 copy-start.1
  83.7 7.6 %multiply_convert_fusion.1 = bf16[768,512]{1,0:T(8,128)(2,1)S(1)} fusion(s32[768,512]{1,0:T(8,128)S(1)} %copy.10, bf16[1,4096,512]{2,1,0:T(8,128)(2,1)} %param.8, bf16[1,768,4096]{2,1,0:T(8,128)(2,1)} %all-gather.13.cloned.1.call-done, f32[512]{0:T(512)S(1)} %bitcast.28, s32[512]{0:T(512)S(1)} %shift_right_arithmetic.26), kind=kOutput, calls=%fused_computation.9 | convolution fusion | flops 3223584768 | bytes 12849152 | tf_op jit(solution)/shard_map/dot_general | solution.py:29
  91.3 0.0 copy-done.1
  91.3 6.4 %fusion.3 = f32[768,4096]{1,0:T(8,128)} fusion(bf16[768,512]{1,0:T(8,128)(2,1)S(1)} %multiply_convert_fusion.1, bf16[1,512,4096]{2,1,0:T(8,128)(2,1)S(1)} %copy-done.1), kind=kOutput, calls=%fused_computation.4 | convolution fusion | flops 3221225472 | bytes 17563648 | tf_op jit(solution)/shard_map/dot_general | solution.py:38
  97.8 0.0 reduce-scatter.2.cloned.1.call-update
  97.8 0.0 copy-start
  97.8 0.0 all-gather.7.cloned.1.call-start
  97.9 139.6 %reduce-scatter.2.cloned.1.call-done = f32[24,4096]{1,0:T(8,128)} async-done(((f32[768,4096]{1,0:T(8,128)}), f32[24,4096]{1,0:T(8,128)}) %reduce-scatter.2.cloned.1.call-update) | async-done | bytes 393232 | tf_op jit(solution)/shard_map/reduce_scatter | solution.py:37
  237.5 10.7 %all-gather.1 = f32[48,4096]{1,0:T(8,128)} all-gather(f32[24,4096]{1,0:T(8,128)} %reduce-scatter.2.cloned.1.call-done), channel_id=3, replica_groups=mesh['layer_0'=4,'layer_1'=2,'lat'=4,'tok'=8] {'layer_1'}, dimensions={0}, use_global_device_ids=true | all-gather | bytes 1179648 | tf_op jit(solution)/shard_map/all_gather | solution.py:13
  248.2 0.0 all-gather.7.cloned.1.call-update
  248.3 0.0 all-gather.9.cloned.1.call-start
  248.3 42.3 %all-gather.7.cloned.1.call-done = f32[8,24,4096]{2,1,0:T(8,128)} async-done(((f32[2,24,4096]{2,1,0:T(8,128)}), f32[8,24,4096]{2,1,0:T(8,128)}) %all-gather.7.cloned.1.call-update) | async-done | bytes 3145744 | tf_op jit(solution)/shard_map/all_gather | solution.py:13
  290.6 2.3 multiply_reduce_fusion.1
  292.9 0.0 copy-done
  292.9 0.9 fusion.10
  293.7 0.0 all-gather.9.cloned.1.call-update
  293.8 0.0 all-gather.11.cloned.1.call-start
  293.8 74.1 %all-gather.9.cloned.1.call-done = f32[8,24,4096]{2,1,0:T(8,128)} async-done(((f32[1,24,4096]{2,1,0:T(8,128)}), f32[8,24,4096]{2,1,0:T(8,128)}) %all-gather.9.cloned.1.call-update) | async-done | bytes 3145744 | tf_op jit(solution)/shard_map/all_gather | solution.py:50
  367.9 2.9 multiply_reduce_fusion
  370.8 0.0 all-gather.11.cloned.1.call-update
  370.9 69.5 %all-gather.11.cloned.1.call-done = bf16[768,4096]{1,0:T(8,128)(2,1)} async-done(((bf16[24,4096]{1,0:T(8,128)(2,1)}), bf16[768,4096]{1,0:T(8,128)(2,1)}) %all-gather.11.cloned.1.call-update) | async-done | bytes 6291472 | tf_op jit(solution)/shard_map/all_gather | solution.py:56
  440.3 7.9 %fusion.2 = bf16[1,512,4096]{2,1,0:T(8,128)(2,1)} fusion(bf16[768,512]{1,0:T(8,128)(2,1)S(1)} %multiply_convert_fusion.1, bf16[768,4096]{1,0:T(8,128)(2,1)} %all-gather.11.cloned.1.call-done), kind=kOutput, calls=%fused_computation.3 | convolution fusion | flops 3225419776 | bytes 11272192 | tf_op jit(solution)/shard_map/dot_general | solution.py:57
  (3 shorter events, 0.0 us)
Async XLA Ops:
  7.2 76.6 %copy-start.2 = (f32[1,512]{1,0:T(1,128)S(1)}, f32[1,512]{1,0:T(1,128)}, u32[]{:S(2)}) copy-start(f32[1,512]{1,0:T(1,128)} %param.9) | copy-start | bytes 6148
  7.2 76.6 %all-gather.13.cloned.1.call-start = ((), (), s32[]{:S(2)}) async-start(), calls=%async_computation.5 | async-start | bytes 6488064 | tf_op jit(solution)/shard_map/all_gather | solution.py:30
  7.9 229.6 %reduce-scatter.2.cloned.1.call-start = ((), (), s32[]{:S(2)}) async-start(), calls=%async_computation.1 | async-start | bytes 12976128 | tf_op jit(solution)/shard_map/reduce_scatter | solution.py:37
  83.7 7.6 %copy-start.1 = (bf16[1,512,4096]{2,1,0:T(8,128)(2,1)S(1)}, bf16[1,512,4096]{2,1,0:T(8,128)(2,1)}, u32[]{:S(2)}) copy-start(bf16[1,512,4096]{2,1,0:T(8,128)(2,1)} %param.11) | copy-start | bytes 12582916
  97.8 195.1 %copy-start = (bf16[1,24,4096]{2,1,0:T(8,128)(2,1)S(1)}, bf16[1,24,4096]{2,1,0:T(8,128)(2,1)}, u32[]{:S(2)}) copy-start(bf16[1,24,4096]{2,1,0:T(8,128)(2,1)} %param.7) | copy-start | bytes 589828
  97.8 192.8 %all-gather.7.cloned.1.call-start = ((), (), s32[]{:S(2)}) async-start(), calls=%async_computation.2 | async-start | bytes 3932160 | tf_op jit(solution)/shard_map/all_gather | solution.py:13
  248.3 119.6 %all-gather.9.cloned.1.call-start = ((), (), s32[]{:S(2)}) async-start(), calls=%async_computation.3 | async-start | bytes 3538944 | tf_op jit(solution)/shard_map/all_gather | solution.py:50
  293.8 146.5 %all-gather.11.cloned.1.call-start = ((), (), s32[]{:S(2)}) async-start(), calls=%async_computation.4 | async-start | bytes 6488064 | tf_op jit(solution)/shard_map/all_gather | solution.py:56
Sparse Core Ops, SparseCore 0:
  10.5 73.1 all-gather.12
  97.9 139.5 reduce-scatter.1
  248.4 42.2 all-gather.6
  293.9 73.9 all-gather.8
  371.0 69.2 all-gather.10
where the time goes:
time: 455 us
  waiting for transfers between devices  400 us (88%)
  matrix products  21.9 us (5%)
  between operations  13.9 us (3%)
  blocking collectives  10.7 us (2%)
  other arithmetic  6.06 us (1%)
    reduce_scatter x1, waiting for transfers between devices, local(): lax.psum_scatter(jnp.dot(latent, weights_out, preferred_element_type=jnp....  140 us
    all_gather x1, waiting for transfers between devices, local(): lax.all_gather(mlp_inputs[0], ('lat', 'tok'), axis=0, tiled=True)  74.2 us
    all_gather x1, waiting for transfers between devices, local(): piece = lax.all_gather(difference[None], LAYER, axis=0, tiled=True)  74.1 us
    all_gather x1, waiting for transfers between devices, local(): gathered = lax.all_gather(signal, ('lat', 'tok'), axis=0, tiled=True)  69.5 us
    all_gather x1, waiting for transfers between devices, whole_of(): nearer = lax.all_gather(x, axes[-1], axis=dim, tiled=True)  42.3 us
    all_gather x1, blocking collectives, whole_of(): nearer = lax.all_gather(x, axes[-1], axis=dim, tiled=True)  10.7 us
  transfers between devices with their start and end apart: 5, of which 5 were waited for; matrix products, arithmetic and copies ran while one was open for 0% of the time, Pallas kernels for 0%

commit v1 on v0

--- a/solution.py
+++ b/solution.py
@@ -47,7 +47,9 @@
     keep = (levels <= layer_index).astype(jnp.float32)
     recon = jnp.sum(piece * keep[:, None, None], axis=0)
     difference = recon - target
-    piece = lax.all_gather(difference[None], LAYER, axis=0, tiled=True)
+    piece = jnp.concatenate(
+        lax.all_to_all(jnp.stack([difference[None]] * lax.axis_size(LAYER)), LAYER, 0, 0), axis=0
+    )
     levels = jnp.arange(piece.shape[0], dtype=jnp.int32)
     keep = (levels >= layer_index).astype(jnp.float32)
     later = jnp.sum(piece * keep[:, None, None], axis=0)

time: 455 us -> 423 us (0.930)
  waiting for transfers between devices: 400 us -> 364 us
    all_gather x1 -> x0, waiting for transfers between devices: 74.1 us -> none  [local(): piece = lax.all_gather(difference[None], LAYER, axis=0, tiled=True)]
    all_to_all x0 -> x1, waiting for transfers between devices: none -> 37.1 us  [local(): lax.all_to_all(jnp.stack([difference[None]] * lax.axis_size(LAYER)), LAYE...]
where the time goes in v1:
time: 423 us
  waiting for transfers between devices  364 us (86%)
  matrix products  22.6 us (5%)
  between operations  13.9 us (3%)
  blocking collectives  10.6 us (3%)
    reduce_scatter x1, waiting for transfers between devices, local(): lax.psum_scatter(jnp.dot(latent, weights_out, preferred_element_type=jnp....  140 us
    all_gather x1, waiting for transfers between devices, local(): lax.all_gather(mlp_inputs[0], ('lat', 'tok'), axis=0, tiled=True)  74.2 us
    all_gather x1, waiting for transfers between devices, local(): gathered = lax.all_gather(signal, ('lat', 'tok'), axis=0, tiled=True)  70.3 us
    all_gather x1, waiting for transfers between devices, whole_of(): nearer = lax.all_gather(x, axes[-1], axis=dim, tiled=True)  42.2 us
    all_to_all x1, waiting for transfers between devices, local(): lax.all_to_all(jnp.stack([difference[None]] * lax.axis_size(LAYER)), LAYE...  37.1 us
    all_gather x1, blocking collectives, whole_of(): nearer = lax.all_gather(x, axes[-1], axis=dim, tiled=True)  10.6 us
    dot_general x1, matrix products, local(): lax.dot_general(latent, gathered, (((0,), (0,)), ((), ())), preferred_ele...  8.56 us
  transfers between devices with their start and end apart: 5, of which 5 were waited for; matrix products, arithmetic and copies ran while one was open for 0% of the time, Pallas kernels for 0%

profile of v1, /device:TPU:1, one launch (start us, length us, event | category | flops | bytes accessed | tf_op | source)
XLA Modules:
  0.0 423.1 jit_solution(4065091434473498682)
XLA Ops:
  7.2 0.0 copy-start.2
  7.2 0.0 all-gather.10.cloned.1.call-start
  7.2 0.7 all-gather.10.cloned.1.call-update
  7.9 0.0 reduce-scatter.2.cloned.1.call-start
  8.0 1.0 shift_right_arithmetic.23
  9.0 0.5 copy.12
  9.5 0.1 shift_right_arithmetic.26
  9.5 74.2 %all-gather.10.cloned.1.call-done = bf16[1,768,4096]{2,1,0:T(8,128)(2,1)} async-done(((bf16[1,24,4096]{2,1,0:T(8,128)(2,1)}), bf16[1,768,4096]{2,1,0:T(8,128)(2,1)}) %all-gather.10.cloned.1.call-update) | async-done | bytes 6291472 | tf_op jit(solution)/shard_map/all_gather | solution.py:30
  83.7 0.0 copy-done.2
  83.7 0.0 copy-start.1
  83.7 7.6 %multiply_convert_fusion.1 = bf16[768,512]{1,0:T(8,128)(2,1)S(1)} fusion(s32[768,512]{1,0:T(8,128)S(1)} %copy.12, bf16[1,4096,512]{2,1,0:T(8,128)(2,1)} %param.8, bf16[1,768,4096]{2,1,0:T(8,128)(2,1)} %all-gather.10.cloned.1.call-done, f32[512]{0:T(512)S(1)} %bitcast.37, s32[512]{0:T(512)S(1)} %shift_right_arithmetic.26), kind=kOutput, calls=%fused_computation.10 | convolution fusion | flops 3223584768 | bytes 12849152 | tf_op jit(solution)/shard_map/dot_general | solution.py:29
  91.3 0.0 copy-done.1
  91.3 0.0 copy-start.3
  91.4 6.4 %fusion.3 = f32[768,4096]{1,0:T(8,128)} fusion(bf16[768,512]{1,0:T(8,128)(2,1)S(1)} %multiply_convert_fusion.1, bf16[1,512,4096]{2,1,0:T(8,128)(2,1)S(1)} %copy-done.1), kind=kOutput, calls=%fused_computation.4 | convolution fusion | flops 3221225472 | bytes 17563648 | tf_op jit(solution)/shard_map/dot_general | solution.py:38
  97.8 0.0 copy-done.3
  97.8 0.0 reduce-scatter.2.cloned.1.call-update
  97.8 0.0 copy-start
  97.8 0.0 all-gather.6.cloned.1.call-start
  97.9 139.9 %reduce-scatter.2.cloned.1.call-done = f32[24,4096]{1,0:T(8,128)} async-done(((f32[768,4096]{1,0:T(8,128)}), f32[24,4096]{1,0:T(8,128)}) %reduce-scatter.2.cloned.1.call-update) | async-done | bytes 393232 | tf_op jit(solution)/shard_map/reduce_scatter | solution.py:37
  237.8 10.6 %all-gather.1 = f32[48,4096]{1,0:T(8,128)} all-gather(f32[24,4096]{1,0:T(8,128)} %reduce-scatter.2.cloned.1.call-done), channel_id=3, replica_groups=mesh['layer_0'=4,'layer_1'=2,'lat'=4,'tok'=8] {'layer_1'}, dimensions={0}, use_global_device_ids=true | all-gather | bytes 1179648 | tf_op jit(solution)/shard_map/all_gather | solution.py:13
  248.4 0.0 all-gather.6.cloned.1.call-update
  248.4 42.2 %all-gather.6.cloned.1.call-done = f32[8,24,4096]{2,1,0:T(8,128)} async-done(((f32[2,24,4096]{2,1,0:T(8,128)}), f32[8,24,4096]{2,1,0:T(8,128)}) %all-gather.6.cloned.1.call-update) | async-done | bytes 3145744 | tf_op jit(solution)/shard_map/all_gather | solution.py:13
  290.7 2.3 multiply_reduce_fusion
  292.9 0.0 copy-done
  292.9 0.7 fusion.11
  293.7 2.0 stack.3
  295.7 3.9 all-to-all-start
  299.6 0.0 all-gather.8.cloned.1.call-start
  299.6 37.1 %all-to-all-done = f32[8,1,24,4096]{3,2,1,0:T(8,128)S(1)} async-done(((f32[8,1,24,4096]{3,2,1,0:T(8,128)}), f32[8,1,24,4096]{3,2,1,0:T(8,128)S(1)}, u32[]{:S(2)}, u32[]{:S(2)}) %all-to-all-start) | async-done | bytes 3145760 | tf_op jit(solution)/shard_map/all_to_all | solution.py:51
  336.8 1.0 fusion.6
  337.7 0.0 all-gather.8.cloned.1.call-update
  337.8 70.3 %all-gather.8.cloned.1.call-done = bf16[768,4096]{1,0:T(8,128)(2,1)} async-done(((bf16[24,4096]{1,0:T(8,128)(2,1)}), bf16[768,4096]{1,0:T(8,128)(2,1)}) %all-gather.8.cloned.1.call-update) | async-done | bytes 6291472 | tf_op jit(solution)/shard_map/all_gather | solution.py:58
  408.0 8.6 %fusion.2 = bf16[1,512,4096]{2,1,0:T(8,128)(2,1)} fusion(bf16[768,512]{1,0:T(8,128)(2,1)} %copy-done.3, bf16[768,4096]{1,0:T(8,128)(2,1)} %all-gather.8.cloned.1.call-done), kind=kOutput, calls=%fused_computation.3 | convolution fusion | flops 3225419776 | bytes 11272192 | tf_op jit(solution)/shard_map/dot_general | solution.py:59
  (3 shorter events, 0.0 us)
Async XLA Ops:
  7.2 76.6 %copy-start.2 = (f32[1,512]{1,0:T(1,128)S(1)}, f32[1,512]{1,0:T(1,128)}, u32[]{:S(2)}) copy-start(f32[1,512]{1,0:T(1,128)} %param.9) | copy-start | bytes 6148
  7.2 76.6 %all-gather.10.cloned.1.call-start = ((), (), s32[]{:S(2)}) async-start(), calls=%async_computation.5 | async-start | bytes 6488064 | tf_op jit(solution)/shard_map/all_gather | solution.py:30
  7.9 229.9 %reduce-scatter.2.cloned.1.call-start = ((), (), s32[]{:S(2)}) async-start(), calls=%async_computation.2 | async-start | bytes 12976128 | tf_op jit(solution)/shard_map/reduce_scatter | solution.py:37
  83.7 7.6 %copy-start.1 = (bf16[1,512,4096]{2,1,0:T(8,128)(2,1)S(1)}, bf16[1,512,4096]{2,1,0:T(8,128)(2,1)}, u32[]{:S(2)}) copy-start(bf16[1,512,4096]{2,1,0:T(8,128)(2,1)} %param.11) | copy-start | bytes 12582916
  91.3 6.4 %copy-start.3 = (bf16[768,512]{1,0:T(8,128)(2,1)}, bf16[768,512]{1,0:T(8,128)(2,1)S(1)}, u32[]{:S(2)}) copy-start(bf16[768,512]{1,0:T(8,128)(2,1)S(1)} %multiply_convert_fusion.1) | copy-start | bytes 2359300
  97.8 195.1 %copy-start = (bf16[1,24,4096]{2,1,0:T(8,128)(2,1)S(1)}, bf16[1,24,4096]{2,1,0:T(8,128)(2,1)}, u32[]{:S(2)}) copy-start(bf16[1,24,4096]{2,1,0:T(8,128)(2,1)} %param.7) | copy-start | bytes 589828
  97.8 192.8 %all-gather.6.cloned.1.call-start = ((), (), s32[]{:S(2)}) async-start(), calls=%async_computation.3 | async-start | bytes 3932160 | tf_op jit(solution)/shard_map/all_gather | solution.py:13
  295.7 41.1 %all-to-all-start = ((f32[8,1,24,4096]{3,2,1,0:T(8,128)}), f32[8,1,24,4096]{3,2,1,0:T(8,128)S(1)}, u32[]{:S(2)}, u32[]{:S(2)}) async-start(f32[8,1,24,4096]{3,2,1,0:T(8,128)} %stack.3), calls=%async_computation.1 | async-start | bytes 6291456 | tf_op jit(solution)/shard_map/all_to_all | solution.py:51
  299.6 108.5 %all-gather.8.cloned.1.call-start = ((), (), s32[]{:S(2)}) async-start(), calls=%async_computation.4 | async-start | bytes 6488064 | tf_op jit(solution)/shard_map/all_gather | solution.py:58
Sparse Core Ops, SparseCore 0:
  10.5 73.1 all-gather.9
  97.9 139.8 reduce-scatter.1
  248.5 42.0 all-gather.5
  337.9 70.1 all-gather.7
